TPU v7x, 8 devices: a whole 2x2x1 slice. The times are simulated.
8 devices in a mesh: rep: 1 (over z), dp: 8 (over x, y, core).
Axes of the slice: x: 2, y: 2, z: 1, core: 2. Of those that a mesh axis runs over, the one named last changes fastest.
Arguments:
- a: bfloat16 [8, 4, 4096, 1024], P(('rep', 'dp'))
- g: bfloat16 [8, 4, 4096, 4096], P(('rep', 'dp'))
Outputs:
- output: bfloat16 [4, 1024, 4096], P('rep')
All inputs are finite; a program needn't handle non-finite values.
Results may differ from a plain program's by a relative error of at most 0.012.
Values are sent between devices in bfloat16 or wider.
A program may use at most 2 GiB of HBM per device.

v0:
```python
import jax
import jax.numpy as jnp


def solution(mesh):
    groups = mesh.shape["rep"]

    def step(a, g):
        a, g = (t.reshape(groups, -1, *t.shape[1:]) for t in (a, g))
        sums = jnp.einsum("rsntd,rsntf->rndf", a, g, preferred_element_type=jnp.float32)
        return sums.astype(jnp.bfloat16).reshape(-1, *sums.shape[2:])

    return step
```

profile of v0, /device:TPU:0, one launch (start us, length us, event | category | flops | bytes accessed | tf_op | source)
XLA Modules:
  0.0 938.0 jit_solution(6306096957104816742)
XLA Ops:
  0.0 150.8 %fusion = f32[4,1024,4096]{2,1,0:T(8,128)} fusion(bf16[1,4,4096,4096]{3,2,1,0:T(8,128)(2,1)} %param.1, bf16[1,4,4096,1024]{3,2,1,0:T(8,128)(2,1)} %param), kind=kOutput, calls=%fused_computation | convolution fusion | flops 137438953472 | bytes 234881024 | tf_op jit(solution)/rsntd,rsntf->rndf/dot_general | solution.py:10
  150.8 787.2 %all-reduce.2 = bf16[4,1024,4096]{2,1,0:T(8,128)(2,1)} all-reduce(f32[4,1024,4096]{2,1,0:T(8,128)} %fusion), channel_id=1, replica_groups=mesh['axis_0'=8] {'axis_0'}, use_global_device_ids=true, to_apply=%add.clone | all-reduce | flops 16777216 | bytes 100663296 | tf_op jit(solution)/rsntd,rsntf->rndf/dot_general | solution.py:10
where the time goes:
time: 938 us
  blocking collectives  787 us (84%)
  matrix products  151 us (16%)
    dot_general x1, blocking collectives, step(): jnp.einsum('rsntd,rsntf->rndf', a, g, preferred_element_type=jnp.float32)  787 us
    dot_general x1, matrix products, step(): jnp.einsum('rsntd,rsntf->rndf', a, g, preferred_element_type=jnp.float32)  151 us

commit v1 on v0

v1 whole, which is shorter than its diff:
```python
import functools

import jax
import jax.numpy as jnp
from jax import lax
from jax.experimental import pallas as pl
from jax.experimental.pallas import tpu as pltpu
from jax.sharding import PartitionSpec as P

MESH = pl.DeviceIdType.MESH
LAG = 2
SLOTS = 4


def flip(i, bit):
    return i + bit - 2 * bit * ((i // bit) % 2)


def kernel(
    cfg, a_ref, g_ref, o_ref,
    a_raw, a_t, g_buf, d2d_out, d2d_in, part, keep1, rs1_out, rs1_in, keep2, rs2_out, rs2_in, done,
    a_sem, g_sem, d2d_s, d2d_r, rs1_s, rs1_r, rs2_s, rs2_r, loc_s, ag1_s, ag1_r, ag2_s, ag2_r, ag3_s, ag3_r,
):
    mats, tokens, d, ff, width, blocks = cfg
    per = ff // width
    steps = mats * per
    half, quarter, eighth = d // 2, d // 4, d // 8
    rows_a = tokens // blocks

    me = lax.axis_index("dp")
    core, y, x = me % 2, (me // 2) % 2, (me // 4) % 2
    cu = x + core * (y - x)
    cv = y + core * (x - y)
    mate = flip(me, 1)
    at_x, at_y = flip(me, 4), flip(me, 2)
    u = at_x + core * (at_y - at_x)
    v = at_y + core * (at_x - at_y)

    mine = pl.multiple_of(core * half, half)
    theirs = pl.multiple_of((1 - core) * half, half)
    q_keep = pl.multiple_of(cu * quarter, quarter)
    q_send = pl.multiple_of((1 - cu) * quarter, quarter)
    e_keep = pl.multiple_of(cv * eighth, eighth)
    e_send = pl.multiple_of((1 - cv) * eighth, eighth)

    def remote(src, dst, s_sem, r_sem, to):
        return pltpu.make_async_remote_copy(
            src_ref=src, dst_ref=dst, send_sem=s_sem, recv_sem=r_sem, device_id={"dp": to}, device_id_type=MESH
        )

    def g_copy(s):
        n, j = s // per, s % per
        cols = pl.ds(pl.multiple_of(j * width, width), width)
        return pltpu.make_async_copy(g_ref.at[0, n, :, cols], g_buf.at[s % 2], g_sem.at[s % 2])

    def a_copy(b):
        n, t = b // blocks, b % blocks
        rows = pl.ds(pl.multiple_of(t * rows_a, rows_a), rows_a)
        return pltpu.make_async_copy(a_ref.at[0, n, rows, :], a_raw.at[b % 2], a_sem.at[b % 2])

    def turn(b):
        a_copy(b).wait()
        n, t = b // blocks, b % blocks
        cols = pl.ds(pl.multiple_of(t * rows_a, rows_a), rows_a)
        a_t[n % 2, :, cols] = a_raw[b % 2].T

        @pl.when(b + 2 < mats * blocks)
        def _():
            a_copy(b + 2).start()

    def region(k, start, rows):
        n, j = k // per, k % per
        return o_ref.at[n, pl.ds(start, rows), pl.ds(pl.multiple_of(j * width, width), width)]

    def d2d(s):
        return remote(d2d_out, d2d_in.at[s % 2], d2d_s.at[0], d2d_r.at[s % 2], mate)

    def rs1(k):
        i = k % SLOTS
        return remote(rs1_out.at[i], rs1_in.at[i], rs1_s.at[i], rs1_r.at[i], u)

    def rs2(k):
        i = k % SLOTS
        return remote(rs2_out.at[i], rs2_in.at[i], rs2_s.at[i], rs2_r.at[i], v)

    e_row = pl.multiple_of(mine + q_keep + e_keep, eighth)
    q_row = pl.multiple_of(mine + q_keep, quarter)

    def local(k):
        i = k % SLOTS
        return pltpu.make_async_copy(done.at[i], region(k, e_row, eighth), loc_s.at[i])

    def ag1(k):
        i = k % SLOTS
        return remote(done.at[i], region(k, e_row, eighth), ag1_s.at[i], ag1_r.at[i], v)

    def ag2(k):
        i = k % SLOTS
        r = region(k, q_row, quarter)
        return remote(r, r, ag2_s.at[i], ag2_r.at[i], u)

    def ag3(k):
        i = k % SLOTS
        r = region(k, mine, half)
        return remote(r, r, ag3_s.at[i], ag3_r.at[i], mate)

    def events(s):
        def on(lag, f):
            k = s - lag
            pl.when(jnp.logical_and(k >= 0, k < steps))(lambda: f(k))

        @functools.partial(on, 5 * LAG)
        def _(k):
            ag3(k).wait()

        @functools.partial(on, 4 * LAG)
        def _(k):
            ag2(k).wait()
            ag3(k).start()

        @functools.partial(on, 3 * LAG)
        def _(k):
            local(k).wait()
            ag1(k).wait()
            ag2(k).start()

        @functools.partial(on, 2 * LAG)
        def _(k):
            rs2(k).wait()
            i = k % SLOTS
            done[i] = (keep2[i] + rs2_in[i].astype(jnp.float32)).astype(jnp.bfloat16)
            ag1(k).start()
            local(k).start()

        @functools.partial(on, LAG)
        def _(k):
            rs1(k).wait()
            i = k % SLOTS
            rows = pl.ds(e_send, eighth)
            rs2_out[i] = (keep1[i, rows, :] + rs1_in[i, rows, :].astype(jnp.float32)).astype(jnp.bfloat16)
            rs2(k).start()
            rows = pl.ds(e_keep, eighth)
            keep2[i] = keep1[i, rows, :] + rs1_in[i, rows, :].astype(jnp.float32)

    a_copy(0).start()
    a_copy(1).start()
    g_copy(0).start()

    barrier = pltpu.get_barrier_semaphore()
    for other in (mate, u, v):
        pl.semaphore_signal(barrier, inc=1, device_id={"dp": other}, device_id_type=MESH)
    pl.semaphore_wait(barrier, 3)

    @pl.loop(0, blocks)
    def _(b):
        turn(b)

    @pl.loop(0, steps)
    def _(s):
        n, j = s // per, s % per
        g_copy(s).wait()

        @pl.when(s + 1 < steps)
        def _():
            g_copy(s + 1).start()

        d2d_out[...] = jnp.dot(
            a_t[n % 2, pl.ds(theirs, half), :], g_buf[s % 2], preferred_element_type=jnp.float32
        ).astype(jnp.bfloat16)
        d2d(s).start()
        events(s)
        part[...] = jnp.dot(a_t[n % 2, pl.ds(mine, half), :], g_buf[s % 2], preferred_element_type=jnp.float32)

        @pl.when(n + 1 < mats)
        def _():
            turn((n + 1) * blocks + j)

        d2d(s).wait()
        i, h = s % SLOTS, s % 2
        rows = pl.ds(q_send, quarter)
        rs1_out[i] = (part[rows, :] + d2d_in[h, rows, :].astype(jnp.float32)).astype(jnp.bfloat16)
        rs1(s).start()
        rows = pl.ds(q_keep, quarter)
        keep1[i] = part[rows, :] + d2d_in[h, rows, :].astype(jnp.float32)

    @pl.loop(steps, steps + 5 * LAG)
    def _(s):
        events(s)


def solution(mesh):
    def step(a, g):
        _, mats, tokens, d = a.shape
        ff = g.shape[-1]
        width = 512 if ff % 512 == 0 else ff
        blocks = ff // width
        half, quarter, eighth = d // 2, d // 4, d // 8
        f32, bf16 = jnp.float32, jnp.bfloat16
        dma = pltpu.SemaphoreType.DMA
        return pl.pallas_call(
            functools.partial(kernel, (mats, tokens, d, ff, width, blocks)),
            out_shape=jax.ShapeDtypeStruct((mats, d, ff), bf16),
            in_specs=[pl.BlockSpec(memory_space=pl.ANY)] * 2,
            out_specs=pl.BlockSpec(memory_space=pl.ANY),
            scratch_shapes=[
                pltpu.VMEM((2, tokens // blocks, d), bf16),
                pltpu.VMEM((2, d, tokens), bf16),
                pltpu.VMEM((2, tokens, width), bf16),
                pltpu.VMEM((half, width), bf16),
                pltpu.VMEM((2, half, width), bf16),
                pltpu.VMEM((half, width), f32),
                pltpu.VMEM((SLOTS, quarter, width), f32),
                pltpu.VMEM((SLOTS, quarter, width), bf16),
                pltpu.VMEM((SLOTS, quarter, width), bf16),
                pltpu.VMEM((SLOTS, eighth, width), f32),
                pltpu.VMEM((SLOTS, eighth, width), bf16),
                pltpu.VMEM((SLOTS, eighth, width), bf16),
                pltpu.VMEM((SLOTS, eighth, width), bf16),
                dma((2,)), dma((2,)), dma((1,)), dma((2,)),
                dma((SLOTS,)), dma((SLOTS,)), dma((SLOTS,)), dma((SLOTS,)), dma((SLOTS,)),
                dma((SLOTS,)), dma((SLOTS,)), dma((SLOTS,)), dma((SLOTS,)), dma((SLOTS,)), dma((SLOTS,)),
            ],
            compiler_params=pltpu.CompilerParams(
                collective_id=0, has_side_effects=True, vmem_limit_bytes=60 * 2**20
            ),
        )(a, g)

    spec = P(("rep", "dp"), None, None, None)
    return jax.shard_map(step, mesh=mesh, in_specs=(spec, spec), out_specs=P("rep", None, None), check_vma=False)
```

time: 938 us -> 316 us (0.34)
  blocking collectives: 787 us -> 0 us
  Pallas kernels: 0 us -> 293 us
  matrix products: 151 us -> 0 us
  local copies, waits for them, and re-layouts: 0 us -> 22.9 us
    dot_general x1 -> x0, blocking collectives: 787 us -> none  [step(): jnp.einsum('rsntd,rsntf->rndf', a, g, preferred_element_type=jnp.float32)]
    pallas_call x0 -> x1, Pallas kernels: none -> 293 us  [step(): pl.pallas_call(functools.partial(kernel, (mats, tokens, d, ff, width, blo...]
    dot_general x1 -> x0, matrix products: 151 us -> none  [step(): jnp.einsum('rsntd,rsntf->rndf', a, g, preferred_element_type=jnp.float32)]
    unnamed x0 -> x1, local copies, waits for them, and re-layouts: none -> 22.9 us
where the time goes in v1:
time: 316 us
  Pallas kernels  293 us (93%)
  local copies, waits for them, and re-layouts  22.9 us (7%)
    pallas_call x1, Pallas kernels, step(): pl.pallas_call(functools.partial(kernel, (mats, tokens, d, ff, width, blo...  293 us
    unnamed x1, local copies, waits for them, and re-layouts  22.9 us

profile of v1, /device:TPU:0, one launch (start us, length us, event | category | flops | bytes accessed | tf_op | source)
XLA Modules:
  0.0 316.1 jit_solution(10579633074117675675)
XLA Ops:
  0.0 293.2 %shard_map.28 = bf16[4,1024,4096]{2,1,0:T(8,128)(2,1)} custom-call(bf16[1,4,4096,1024]{3,2,1,0:T(8,128)(2,1)} %a_ref.1, bf16[1,4,4096,4096]{3,2,1,0:T(8,128)(2,1)} %g_ref.1), custom_call_target="tpu_custom_call" | custom-call | tf_op jit(solution)/shard_map/pallas_call | solution.py:200
  293.2 22.9 %copy.4 = bf16[4,1024,4096]{2,1,0:T(8,128)(2,1)} copy(bf16[4,1024,4096]{2,1,0:T(8,128)(2,1)} %shard_map.28) | data formatting | bytes 67108864

commit v2 on v0

v2 whole, which is shorter than its diff:
```python
import functools

import jax
import jax.numpy as jnp
from jax import lax
from jax.experimental import pallas as pl
from jax.experimental.pallas import tpu as pltpu
from jax.sharding import PartitionSpec as P

MESH = pl.DeviceIdType.MESH
SLOTS = 4
HELD = 8
RAW = 4
RS1, RS2, AG1, AG2, AG3 = 1, 2, 3, 5, 6


def flip(i, bit):
    return i + bit - 2 * bit * ((i // bit) % 2)


def kernel(
    cfg, a_ref, g_ref, o_ref,
    a_raw, a_t, g_buf, d2d_out, d2d_in, part, keep1, rs1_out, rs1_in, keep2, rs2_out, rs2_in,
    a_sem, g_sem, g0_sem, d2d_s, d2d_r, rs1_s, rs1_r, rs2_s, rs2_r, ag1_s, ag1_r, ag2_s, ag2_r, ag3_s, ag3_r,
):
    mats, tokens, d, ff, width, blocks = cfg
    per = ff // width
    steps = mats * per
    half, quarter, eighth = d // 2, d // 4, d // 8
    rows_a = tokens // blocks
    f32, bf16 = jnp.float32, jnp.bfloat16

    me = lax.axis_index("dp")
    core, y, x = me % 2, (me // 2) % 2, (me // 4) % 2
    cu = x + core * (y - x)
    cv = y + core * (x - y)
    mate = flip(me, 1)
    at_x, at_y = flip(me, 4), flip(me, 2)
    u = at_x + core * (at_y - at_x)
    v = at_y + core * (at_x - at_y)

    mine = pl.multiple_of(core * half, half)
    theirs = pl.multiple_of((1 - core) * half, half)
    q_keep = pl.ds(pl.multiple_of(cu * quarter, quarter), quarter)
    q_send = pl.ds(pl.multiple_of((1 - cu) * quarter, quarter), quarter)
    e_keep = pl.ds(pl.multiple_of(cv * eighth, eighth), eighth)
    e_send = pl.ds(pl.multiple_of((1 - cv) * eighth, eighth), eighth)
    rows_h = pl.ds(mine, half)
    rows_send = pl.ds(pl.multiple_of(mine + (1 - cu) * quarter, quarter), quarter)
    rows_q = pl.ds(pl.multiple_of(mine + cu * quarter, quarter), quarter)
    rows_e = pl.ds(pl.multiple_of(mine + cu * quarter + cv * eighth, eighth), eighth)

    def remote(src, dst, s_sem, r_sem, to):
        return pltpu.make_async_remote_copy(
            src_ref=src, dst_ref=dst, send_sem=s_sem, recv_sem=r_sem, device_id={"dp": to}, device_id_type=MESH
        )

    part_w = width // 2

    def cols(k):
        return pl.ds(pl.multiple_of((k % per) * width, width), width)

    def cols_of(k, p):
        return pl.ds(pl.multiple_of((k % per) * width + p * part_w, part_w), part_w)

    def lanes(p):
        return pl.ds(p * part_w, part_w)

    def g_copy(s):
        return pltpu.make_async_copy(g_ref.at[0, s // per, :, cols(s)], g_buf.at[s % 2], g_sem.at[s % 2])

    def g_first(b):
        rows = pl.ds(b * rows_a, rows_a)
        return pltpu.make_async_copy(g_ref.at[0, 0, rows, pl.ds(0, width)], g_buf.at[0, rows, :], g0_sem.at[b])

    def a_copy(b):
        rows = pl.ds(pl.multiple_of((b % blocks) * rows_a, rows_a), rows_a)
        return pltpu.make_async_copy(a_ref.at[0, b // blocks, rows, :], a_raw.at[b % RAW], a_sem.at[b % RAW])

    def d2d(s):
        return remote(d2d_out, d2d_in.at[s % 2], d2d_s.at[0], d2d_r.at[s % 2], mate)

    def rs1(k, p):
        i, j = k % SLOTS, k % SLOTS * 2 + p
        return remote(rs1_out.at[i, :, lanes(p)], rs1_in.at[i, :, lanes(p)], rs1_s.at[j], rs1_r.at[j], u)

    def rs2(k, p):
        i, j = k % SLOTS, k % SLOTS * 2 + p
        return remote(rs2_out.at[i, :, lanes(p)], rs2_in.at[i, :, lanes(p)], rs2_s.at[j], rs2_r.at[j], v)

    def gather(k, p, rows, s_sem, r_sem, to):
        j = k % HELD * 2 + p
        r = o_ref.at[k // per, rows, cols_of(k, p)]
        return remote(r, r, s_sem.at[j], r_sem.at[j], to)

    def ag1(k, p):
        return gather(k, p, rows_e, ag1_s, ag1_r, v)

    def ag2(k, p):
        return gather(k, p, rows_q, ag2_s, ag2_r, u)

    def ag3(k, p):
        return gather(k, p, rows_h, ag3_s, ag3_r, mate)

    def at(s, lag):
        def run(f):
            k = s - lag
            pl.when(jnp.logical_and(k >= 0, k < steps))(lambda: f(k))
        return run

    def events(s, p):
        c = lanes(p)

        @at(s, AG3)
        def _(k):
            ag3(k, p).wait()

        @at(s, AG2)
        def _(k):
            ag2(k, p).wait()
            ag3(k, p).start()

        @at(s, AG1)
        def _(k):
            ag1(k, p).wait()
            ag2(k, p).start()

        @at(s, RS2)
        def _(k):
            rs2(k, p).wait()
            i = k % SLOTS
            o_ref[k // per, rows_e, cols_of(k, p)] = (keep2[i, :, c] + rs2_in[i, :, c].astype(f32)).astype(bf16)
            ag1(k, p).start()

        @at(s, RS1)
        def _(k):
            rs1(k, p).wait()
            i = k % SLOTS
            rs2_out[i, :, c] = (keep1[i, e_send, c] + rs1_in[i, e_send, c].astype(f32)).astype(bf16)
            rs2(k, p).start()
            keep2[i, :, c] = keep1[i, e_keep, c] + rs1_in[i, e_keep, c].astype(f32)

    def pair(s):
        d2d(s).wait()
        i, h = s % SLOTS, s % 2
        for p in range(2):
            c = lanes(p)
            rs1_out[i, :, c] = (part[rows_send, c] + d2d_in[h, q_send, c].astype(f32)).astype(bf16)
            rs1(s, p).start()
        keep1[i] = part[rows_q, :] + d2d_in[h, q_keep, :].astype(f32)

    def dot(rows, s):
        return jnp.dot(a_t[pl.ds(rows, half), :], g_buf[s % 2], preferred_element_type=f32)

    for b in range(RAW):
        a_copy(b).start()
        g_first(b).start()

    barrier = pltpu.get_barrier_semaphore()
    for peer in (mate, u, v):
        pl.semaphore_signal(barrier, inc=1, device_id={"dp": peer}, device_id_type=MESH)

    for b in range(blocks + 1):
        if b < blocks:
            a_copy(b).wait()
        if b >= 1:
            g_first(b - 1).wait()
        if b < blocks:
            a_t[:, b * rows_a:(b + 1) * rows_a] = a_raw[b % RAW].T
        if b >= 1:
            k = slice((b - 1) * rows_a, b * rows_a)
            new = jnp.dot(a_t[:, k], g_buf[0, k, :], preferred_element_type=f32)
            part[...] = new if b == 1 else part[...] + new
        if b + RAW < blocks:
            g_first(b + RAW).start()
        if b < blocks:
            a_copy(b + RAW).start()
        if b == blocks - 1:
            g_copy(1).start()
    d2d_out[...] = part[pl.ds(theirs, half), :].astype(bf16)
    pl.semaphore_wait(barrier, 3)
    d2d(0).start()
    pair(0)

    @pl.loop(1, steps)
    def _(s):
        @pl.when(s % per == 0)
        def _():
            @pl.loop(s // per * blocks, s // per * blocks + blocks)
            def _(b):
                a_copy(b).wait()
                a_t[:, pl.ds(pl.multiple_of((b % blocks) * rows_a, rows_a), rows_a)] = a_raw[b % RAW].T
                pl.when(b + RAW < mats * blocks)(lambda: a_copy(b + RAW).start())

        g_copy(s).wait()
        pl.when(s + 1 < steps)(lambda: g_copy(s + 1).start())
        d2d_out[...] = dot(theirs, s).astype(bf16)
        d2d(s).start()
        events(s, 0)
        part[pl.ds(mine, half), :] = dot(mine, s)
        pair(s)
        events(s, 1)

    @pl.loop(steps, steps + AG3 + 1)
    def _(s):
        events(s, 0)
        events(s, 1)


def spread(held, o_ref, sem):
    mats, d, _ = o_ref.shape
    pieces = sem.shape[0] // mats
    rows = d // pieces
    copies = []
    for i in range(mats * pieces):
        at = (i // pieces, pl.ds(i % pieces * rows, rows))
        copies.append(pltpu.make_async_copy(held.at[at], o_ref.at[at], sem.at[i]))
    for c in copies:
        c.start()
    for c in copies:
        c.wait()


def solution(mesh):
    def step(a, g):
        _, mats, tokens, d = a.shape
        ff = g.shape[-1]
        width = 512 if ff % 512 == 0 else ff
        blocks = ff // width
        half, quarter, eighth = d // 2, d // 4, d // 8
        f32, bf16 = jnp.float32, jnp.bfloat16
        dma = pltpu.SemaphoreType.DMA
        held = pl.pallas_call(
            functools.partial(kernel, (mats, tokens, d, ff, width, blocks)),
            out_shape=pltpu.VMEM((mats, d, ff), bf16),
            in_specs=[pl.BlockSpec(memory_space=pl.ANY)] * 2,
            out_specs=pl.BlockSpec(memory_space=pltpu.VMEM),
            scratch_shapes=[
                pltpu.VMEM((RAW, tokens // blocks, d), bf16),
                pltpu.VMEM((d, tokens), bf16),
                pltpu.VMEM((2, tokens, width), bf16),
                pltpu.VMEM((half, width), bf16),
                pltpu.VMEM((2, half, width), bf16),
                pltpu.VMEM((d, width), f32),
                pltpu.VMEM((SLOTS, quarter, width), f32),
                pltpu.VMEM((SLOTS, quarter, width), bf16),
                pltpu.VMEM((SLOTS, quarter, width), bf16),
                pltpu.VMEM((SLOTS, eighth, width), f32),
                pltpu.VMEM((SLOTS, eighth, width), bf16),
                pltpu.VMEM((SLOTS, eighth, width), bf16),
                dma((RAW,)), dma((2,)), dma((blocks,)), dma((1,)), dma((2,)),
                *[dma((2 * SLOTS,)) for _ in range(4)], *[dma((2 * HELD,)) for _ in range(6)],
            ],
            compiler_params=pltpu.CompilerParams(
                collective_id=0, has_side_effects=True, vmem_limit_bytes=31 * 2**20 + 2**19
            ),
        )(a, g)
        return pl.pallas_call(
            spread,
            out_shape=jax.ShapeDtypeStruct((mats, d, ff), bf16),
            in_specs=[pl.BlockSpec(memory_space=pltpu.VMEM)],
            out_specs=pl.BlockSpec(memory_space=pl.ANY),
            scratch_shapes=[dma((4 * mats,))],
            compiler_params=pltpu.CompilerParams(vmem_limit_bytes=2**20),
        )(held)

    spec = P(("rep", "dp"), None, None, None)
    return jax.shard_map(step, mesh=mesh, in_specs=(spec, spec), out_specs=P("rep", None, None), check_vma=False)
```

time: 938 us -> 300 us (0.32)
  blocking collectives: 787 us -> 0 us
  Pallas kernels: 0 us -> 300 us
  matrix products: 151 us -> 0 us
    dot_general x1 -> x0, blocking collectives: 787 us -> none  [step(): jnp.einsum('rsntd,rsntf->rndf', a, g, preferred_element_type=jnp.float32)]
    pallas_call x0 -> x2, Pallas kernels: none -> 300 us  [the longest x1 289 us: step(): pl.pallas_call(functools.partial(kernel, (mats, tokens, d, ff, width, blo...]
    dot_general x1 -> x0, matrix products: 151 us -> none  [step(): jnp.einsum('rsntd,rsntf->rndf', a, g, preferred_element_type=jnp.float32)]
where the time goes in v2:
time: 300 us
  Pallas kernels  300 us (100%)
    pallas_call x1, Pallas kernels, step(): pl.pallas_call(functools.partial(kernel, (mats, tokens, d, ff, width, blo...  289 us
    pallas_call x1, Pallas kernels, step(): pl.pallas_call(spread, out_shape=jax.ShapeDtypeStruct((mats, d, ff), bf16...  11 us

profile of v2, /device:TPU:0, one launch (start us, length us, event | category | flops | bytes accessed | tf_op | source)
XLA Modules:
  0.0 299.7 jit_solution(7505827789942859385)
XLA Ops:
  0.0 288.7 %shard_map.28.held = bf16[4,1024,4096]{2,1,0:T(8,128)(2,1)S(1)} custom-call(bf16[1,4,4096,1024]{3,2,1,0:T(8,128)(2,1)} %a_ref.1, bf16[1,4,4096,4096]{3,2,1,0:T(8,128)(2,1)} %g_ref.1), custom_call_target="tpu_custom_call" | custom-call | tf_op jit(solution)/shard_map/pallas_call | solution.py:233
  288.7 11.0 %shard_map.29 = bf16[4,1024,4096]{2,1,0:T(8,128)(2,1)} custom-call(bf16[4,1024,4096]{2,1,0:T(8,128)(2,1)S(1)} %shard_map.28.held), custom_call_target="tpu_custom_call" | custom-call | tf_op jit(solution)/shard_map/pallas_call | solution.py:258

commit v3 on v2

v3 whole, which is shorter than its diff:
```python
import functools

import jax
import jax.numpy as jnp
from jax import lax
from jax.experimental import pallas as pl
from jax.experimental.pallas import tpu as pltpu
from jax.sharding import PartitionSpec as P

MESH = pl.DeviceIdType.MESH
SLOTS = 4
HELD = 8
TAIL = 4
RAW = 4
RS1, RS2, AG1, AG2, AG3 = 1, 2, 3, 5, 6


def flip(i, bit):
    return i + bit - 2 * bit * ((i // bit) % 2)


def kernel(
    cfg, a_ref, g_ref, o_ref, tail_ref,
    a_raw, a_t, g_buf, d2d_out, d2d_in, part, keep1, rs1_out, rs1_in, keep2, rs2_out, rs2_in,
    a_sem, g_sem, g0_sem, d2d_s, d2d_r, rs1_s, rs1_r, rs2_s, rs2_r, ag1_s, ag1_r, ag2_s, ag2_r, ag3_s, ag3_r,
):
    mats, tokens, d, ff, width, blocks = cfg
    per = ff // width
    steps = mats * per
    half, quarter, eighth = d // 2, d // 4, d // 8
    rows_a = tokens // blocks
    f32, bf16 = jnp.float32, jnp.bfloat16

    me = lax.axis_index("dp")
    core, y, x = me % 2, (me // 2) % 2, (me // 4) % 2
    cu = x + core * (y - x)
    cv = y + core * (x - y)
    mate = flip(me, 1)
    at_x, at_y = flip(me, 4), flip(me, 2)
    u = at_x + core * (at_y - at_x)
    v = at_y + core * (at_x - at_y)

    mine = pl.multiple_of(core * half, half)
    theirs = pl.multiple_of((1 - core) * half, half)
    e_keep = pl.ds(pl.multiple_of(cv * eighth, eighth), eighth)
    e_send = pl.ds(pl.multiple_of((1 - cv) * eighth, eighth), eighth)
    rows_h = pl.ds(mine, half)
    order = (
        theirs + (1 - cv) * quarter, mine + (1 - cu) * quarter, theirs + cv * quarter, mine + cu * quarter
    )
    send_theirs, send_mine, keep_theirs, keep_mine = (pl.ds(i * quarter, quarter) for i in range(4))
    rows_q = pl.ds(pl.multiple_of(mine + cu * quarter, quarter), quarter)
    e_keep = pl.ds(pl.multiple_of(cv * eighth, eighth), eighth)
    e_send = pl.ds(pl.multiple_of((1 - cv) * eighth, eighth), eighth)
    rows_h = pl.ds(mine, half)
    rows_send = pl.ds(pl.multiple_of(mine + (1 - cu) * quarter, quarter), quarter)
    rows_mate = [pl.ds(pl.multiple_of(theirs + c * quarter, quarter), quarter) for c in (1 - cv, cv)]
    rows_q = pl.ds(pl.multiple_of(mine + cu * quarter, quarter), quarter)
    rows_e = pl.ds(pl.multiple_of(mine + cu * quarter + cv * eighth, eighth), eighth)

    def remote(src, dst, s_sem, r_sem, to):
        return pltpu.make_async_remote_copy(
            src_ref=src, dst_ref=dst, send_sem=s_sem, recv_sem=r_sem, device_id={"dp": to}, device_id_type=MESH
        )

    part_w = width // 2

    def cols(k):
        return pl.ds(pl.multiple_of((k % per) * width, width), width)

    def cols_of(k, p):
        return pl.ds(pl.multiple_of((k % per) * width + p * part_w, part_w), part_w)

    def lanes(p):
        return pl.ds(p * part_w, part_w)

    def g_copy(s):
        return pltpu.make_async_copy(g_ref.at[0, s // per, :, cols(s)], g_buf.at[s % 2], g_sem.at[s % 2])

    def g_first(b):
        rows = pl.ds(b * rows_a, rows_a)
        return pltpu.make_async_copy(g_ref.at[0, 0, rows, pl.ds(0, width)], g_buf.at[0, rows, :], g0_sem.at[b])

    class a_copy:
        def __init__(self, b, f):
            i = b % RAW
            rows = pl.ds(pl.multiple_of((b % blocks) * rows_a, rows_a), rows_a)
            self.copies = [
                pltpu.make_async_copy(
                    a_ref.at[0, b // blocks, rows, pl.ds(pl.multiple_of(order[2 * f + c], quarter), quarter)],
                    a_raw.at[f, i, :, pl.ds(c * quarter, quarter)],
                    a_sem.at[(2 * f + c) * RAW + i],
                )
                for c in range(2)
            ]

        def start(self):
            for c in self.copies:
                c.start()

        def wait(self):
            for c in self.copies:
                c.wait()

    def d2d(s, q):
        i = s % 2
        return remote(d2d_out.at[q], d2d_in.at[i, q], d2d_s.at[q], d2d_r.at[i * 2 + q], mate)

    def rs1(k, p):
        i, j = k % SLOTS, k % SLOTS * 2 + p
        return remote(rs1_out.at[i, :, lanes(p)], rs1_in.at[i, :, lanes(p)], rs1_s.at[j], rs1_r.at[j], u)

    def rs2(k, p):
        i, j = k % SLOTS, k % SLOTS * 2 + p
        return remote(rs2_out.at[i, :, lanes(p)], rs2_in.at[i, :, lanes(p)], rs2_s.at[j], rs2_r.at[j], v)

    def gather(k, p, rows, s_sem, r_sem, to):
        j = k % HELD * 2 + p
        r = o_ref.at[k // per, rows, cols_of(k, p)]
        return remote(r, r, s_sem.at[j], r_sem.at[j], to)

    def ag1(k, p):
        return gather(k, p, rows_e, ag1_s, ag1_r, v)

    def ag2(k, p):
        return gather(k, p, rows_q, ag2_s, ag2_r, u)

    def ag3(k, p):
        return gather(k, p, rows_h, ag3_s, ag3_r, mate)

    def at(s, lag, end=steps):
        def run(f):
            k = s - lag
            pl.when(jnp.logical_and(k >= 0, k < end))(lambda: f(k))
        return run

    def events(s, p):
        c = lanes(p)

        @at(s, AG3, steps - (TAIL + p) // 2)
        def _(k):
            ag3(k, p).wait()

        @at(s, AG2, steps - (TAIL + p) // 2)
        def _(k):
            ag2(k, p).wait()
            ag3(k, p).start()

        @at(s, AG1)
        def _(k):
            ag1(k, p).wait()
            tail = 2 * (k - steps) + p + TAIL
            pl.when(tail < 0)(lambda: ag2(k, p).start())

            @pl.when(tail >= 0)
            def _():
                to = pl.ds(pl.multiple_of(tail * part_w, part_w), part_w)
                tail_ref[:, to] = o_ref[mats - 1, rows_q, cols_of(k, p)]

        @at(s, RS2)
        def _(k):
            rs2(k, p).wait()
            i = k % SLOTS
            o_ref[k // per, rows_e, cols_of(k, p)] = (keep2[i, :, c] + rs2_in[i, :, c].astype(f32)).astype(bf16)
            ag1(k, p).start()

        @at(s, RS1)
        def _(k):
            rs1(k, p).wait()
            i = k % SLOTS
            rs2_out[i, :, c] = (keep1[i, e_send, c] + rs1_in[i, e_send, c].astype(f32)).astype(bf16)
            rs2(k, p).start()
            keep2[i, :, c] = keep1[i, e_keep, c] + rs1_in[i, e_keep, c].astype(f32)

    def send_on(s, product):
        d2d(s, 0).wait()
        i, h = s % SLOTS, s % 2
        rs1_out[i] = (product() + d2d_in[h, 0].astype(f32)).astype(bf16)
        for p in range(2):
            rs1(s, p).start()

    def keep(s, product):
        d2d(s, 1).wait()
        i, h = s % SLOTS, s % 2
        keep1[i] = product() + d2d_in[h, 1].astype(f32)

    for b in range(RAW):
        a_copy(b, 0).start()
        g_first(b).start()

    barrier = pltpu.get_barrier_semaphore()
    for peer in (mate, u, v):
        pl.semaphore_signal(barrier, inc=1, device_id={"dp": peer}, device_id_type=MESH)

    for f in range(2):
        to = slice(2 * f * quarter, 2 * (f + 1) * quarter)
        for b in range(blocks + 1):
            if b < blocks:
                a_copy(b, f).wait()
            if b >= 1 and f == 0:
                g_first(b - 1).wait()
            if b < blocks:
                a_t[to, b * rows_a:(b + 1) * rows_a] = a_raw[f, b % RAW].T
            if b >= 1:
                k = slice((b - 1) * rows_a, b * rows_a)
                new = jnp.dot(a_t[to, k], g_buf[0, k, :], preferred_element_type=f32)
                part[to, :] = new if b == 1 else part[to, :] + new
            if b + RAW < blocks:
                a_copy(b + RAW, f).start()
                if f == 0:
                    g_first(b + RAW).start()
            elif b < blocks:
                if f == 0:
                    a_copy(b + RAW - blocks, 1).start()
                else:
                    a_copy(b + RAW, 0).start()
                    a_copy(b + RAW, 1).start()
            if f == 1 and b == blocks // 2:
                g_copy(1).start()
                send_on(0, lambda: part[send_mine, :])
        if f == 0:
            pl.semaphore_wait(barrier, 3)
        d2d_out[f] = part[(send_theirs, keep_theirs)[f], :].astype(bf16)
        d2d(0, f).start()

    @pl.loop(1, steps)
    def _(s):
        @pl.when(s % per == 0)
        def _():
            @pl.loop(s // per * blocks, s // per * blocks + blocks)
            def _(b):
                for f in range(2):
                    a_copy(b, f).wait()
                    blk = pl.ds(pl.multiple_of((b % blocks) * rows_a, rows_a), rows_a)
                    a_t[2 * f * quarter:2 * (f + 1) * quarter, blk] = a_raw[f, b % RAW].T
                    pl.when(b + RAW < mats * blocks)(lambda: a_copy(b + RAW, f).start())

        g_copy(s).wait()
        pl.when(s + 1 < steps)(lambda: g_copy(s + 1).start())
        def product(rows):
            return jnp.dot(a_t[rows, :], g_buf[s % 2], preferred_element_type=f32)

        d2d_out[0] = product(send_theirs).astype(bf16)
        d2d(s, 0).start()
        pl.when(s == 1)(lambda: keep(0, lambda: part[keep_mine, :]))
        d2d_out[1] = product(keep_theirs).astype(bf16)
        d2d(s, 1).start()
        events(s, 0)
        send_on(s, lambda: product(send_mine))
        keep(s, lambda: product(keep_mine))
        events(s, 1)

    @pl.loop(steps, steps + AG3 + 1)
    def _(s):
        events(s, 0)
        events(s, 1)


def place(me, d):
    half, quarter = d // 2, d // 4
    core, y, x = me % 2, (me // 2) % 2, (me // 4) % 2
    cu, cv = x + core * (y - x), y + core * (x - y)
    starts = (
        core * half + cu * quarter, core * half + (1 - cu) * quarter,
        (1 - core) * half + cv * quarter, (1 - core) * half + (1 - cv) * quarter,
    )
    return [pl.ds(pl.multiple_of(i, quarter), quarter) for i in starts]


def spread(tail, held, o_ref, sem):
    mats, d, ff = o_ref.shape
    own = place(lax.axis_index("dp"), d)[0]
    parts = [(n, pl.ds(i * (d // 4), d // 4), pl.ds(0, ff)) for n in range(mats - 1) for i in range(4)]
    parts += [(mats - 1, pl.ds(i * (d // 4), d // 4), pl.ds(0, ff - tail)) for i in range(4)]
    parts += [(mats - 1, own, pl.ds(ff - tail, tail))]
    copies = [pltpu.make_async_copy(held.at[p], o_ref.at[p], sem.at[i]) for i, p in enumerate(parts)]
    for c in copies:
        c.start()
    for c in copies:
        c.wait()


def finish(from_u, from_mate, from_far, _, o_ref, sem):
    mats, d, ff = o_ref.shape
    tail = from_u.shape[1]
    rows = place(lax.axis_index("dp"), d)[1:]
    copies = [
        pltpu.make_async_copy(piece, o_ref.at[mats - 1, r, pl.ds(ff - tail, tail)], sem.at[i])
        for i, (piece, r) in enumerate(zip((from_u, from_mate, from_far), rows))
    ]
    for c in copies:
        c.start()
    for c in copies:
        c.wait()


def solution(mesh):
    def step(a, g):
        _, mats, tokens, d = a.shape
        ff = g.shape[-1]
        width = 512 if ff % 512 == 0 else ff
        blocks = ff // width
        half, quarter, eighth = d // 2, d // 4, d // 8
        f32, bf16 = jnp.float32, jnp.bfloat16
        dma = pltpu.SemaphoreType.DMA
        tail = TAIL * width // 2
        held, quarters = pl.pallas_call(
            functools.partial(kernel, (mats, tokens, d, ff, width, blocks)),
            out_shape=(pltpu.VMEM((mats, d, ff), bf16), pltpu.VMEM((quarter, tail), bf16)),
            in_specs=[pl.BlockSpec(memory_space=pl.ANY)] * 2,
            out_specs=(pl.BlockSpec(memory_space=pltpu.VMEM), pl.BlockSpec(memory_space=pltpu.VMEM)),
            scratch_shapes=[
                pltpu.VMEM((2, RAW, tokens // blocks, half), bf16),
                pltpu.VMEM((d, tokens), bf16),
                pltpu.VMEM((2, tokens, width), bf16),
                pltpu.VMEM((2, quarter, width), bf16),
                pltpu.VMEM((2, 2, quarter, width), bf16),
                pltpu.VMEM((d, width), f32),
                pltpu.VMEM((SLOTS, quarter, width), f32),
                pltpu.VMEM((SLOTS, quarter, width), bf16),
                pltpu.VMEM((SLOTS, quarter, width), bf16),
                pltpu.VMEM((SLOTS, eighth, width), f32),
                pltpu.VMEM((SLOTS, eighth, width), bf16),
                pltpu.VMEM((SLOTS, eighth, width), bf16),
                dma((4 * RAW,)), dma((2,)), dma((blocks,)), dma((2,)), dma((4,)),
                *[dma((2 * SLOTS,)) for _ in range(4)], *[dma((2 * HELD,)) for _ in range(6)],
            ],
            compiler_params=pltpu.CompilerParams(
                collective_id=0, has_side_effects=True, vmem_limit_bytes=31 * 2**20
            ),
        )(a, g)
        devices = range(mesh.shape["dp"])
        near = [flip(i, 2 if i % 2 else 4) for i in devices]
        send = lambda to: lax.ppermute(quarters, "dp", [(i, to[i]) for i in devices])
        from_u = send(near)
        from_far = send([flip(i, 1) for i in near])
        from_mate = send([flip(i, 1) for i in devices])
        whole = jax.ShapeDtypeStruct((mats, d, ff), bf16)
        out = pl.pallas_call(
            functools.partial(spread, tail),
            out_shape=whole,
            in_specs=[pl.BlockSpec(memory_space=pltpu.VMEM)],
            out_specs=pl.BlockSpec(memory_space=pl.ANY),
            scratch_shapes=[dma((4 * mats + 1,))],
            compiler_params=pltpu.CompilerParams(vmem_limit_bytes=2**20),
            cost_estimate=pl.CostEstimate(flops=10**10, bytes_accessed=2 * mats * d * ff * 2, transcendentals=0),
        )(held)
        return pl.pallas_call(
            finish,
            out_shape=whole,
            in_specs=[pl.BlockSpec(memory_space=pltpu.VMEM)] * 3 + [pl.BlockSpec(memory_space=pl.ANY)],
            out_specs=pl.BlockSpec(memory_space=pl.ANY),
            scratch_shapes=[dma((3,))],
            input_output_aliases={3: 0},
            compiler_params=pltpu.CompilerParams(vmem_limit_bytes=8 * 2**20),
        )(from_u, from_mate, from_far, out)

    spec = P(("rep", "dp"), None, None, None)
    return jax.shard_map(step, mesh=mesh, in_specs=(spec, spec), out_specs=P("rep", None, None), check_vma=False)
```

time: 300 us -> 297 us (0.990)
  Pallas kernels: 300 us -> 293 us
  starting transfers between devices: 0 us -> 3.45 us
    pallas_call x1, Pallas kernels: 289 us -> 281 us  [step(): pl.pallas_call(functools.partial(kernel, (mats, tokens, d, ff, width, blo...]
    ppermute x0 -> x3, starting transfers between devices: none -> 3.45 us  [step(): lax.ppermute(quarters, 'dp', [(i, to[i]) for i in devices])]
    pallas_call x1 -> x2, Pallas kernels: 11 us -> 11.7 us  [the longest x1 10.5 us: step(): pl.pallas_call(functools.partial(spread, tail), out_shape=whole, in_specs...]
  transfers between devices with their start and end apart: 0 -> 3, of which waited for: 0 -> 1; matrix products, arithmetic and copies ran while one was open for 0% -> 0% of each run, Pallas kernels for 0% -> 4%
where the time goes in v3:
time: 297 us
  Pallas kernels  293 us (99%)
  starting transfers between devices  3.45 us (1%)
    pallas_call x1, Pallas kernels, step(): pl.pallas_call(functools.partial(kernel, (mats, tokens, d, ff, width, blo...  281 us
    pallas_call x1, Pallas kernels, step(): pl.pallas_call(functools.partial(spread, tail), out_shape=whole, in_specs...  10.5 us
  transfers between devices with their start and end apart: 3, of which 1 were waited for; matrix products, arithmetic and copies ran while one was open for 0% of the time, Pallas kernels for 4%

profile of v3, /device:TPU:0, one launch (start us, length us, event | category | flops | bytes accessed | tf_op | source)
XLA Modules:
  0.0 296.7 jit_solution(16743137740519596821)
XLA Ops:
  0.0 280.8 %shard_map.28 = (bf16[4,1024,4096]{2,1,0:T(8,128)(2,1)S(1)}, bf16[256,1024]{1,0:T(8,128)(2,1)S(1)}) custom-call(bf16[1,4,4096,1024]{3,2,1,0:T(8,128)(2,1)} %a_ref.1, bf16[1,4,4096,4096]{3,2,1,0:T(8,128)(2,1)} %g_ref.1), custom_call_target="tpu_custom_call" | custom-call | tf_op jit(solution)/shard_map/pallas_call | solution.py:307
  280.8 1.2 collective-permute-start.2
  282.0 0.6 collective-permute-start.1
  282.6 1.7 collective-permute-start
  284.3 10.5 %shard_map.29._ = bf16[4,1024,4096]{2,1,0:T(8,128)(2,1)} custom-call(bf16[4,1024,4096]{2,1,0:T(8,128)(2,1)S(1)} %get-tuple-element.8.held), custom_call_target="tpu_custom_call" | custom-call | flops 10000000000 | bytes 67108864 | tf_op jit(solution)/shard_map/pallas_call | solution.py:339
  294.8 0.0 collective-permute-done.2.from_far
  294.8 0.0 collective-permute-done.1.from_mate
  294.8 0.7 collective-permute-done.from_u
  295.5 1.2 shard_map.30
Async XLA Ops:
  280.8 14.0 %collective-permute-start.2 = (bf16[256,1024]{1,0:T(8,128)(2,1)S(1)}, bf16[256,1024]{1,0:T(8,128)(2,1)S(1)}, u32[]{:S(2)}, u32[]{:S(2)}) collective-permute-start(bf16[256,1024]{1,0:T(8,128)(2,1)S(1)} %get-tuple-element.7), channel_id=1, source_target_pairs={{0,5},{1,2},{2,7},{3,0},{4,1},{5,6},{6,3},{7,4}} | collective-permute-start | bytes 1572872 | tf_op jit(solution)/shard_map/ppermute | solution.py:334
  282.0 12.8 %collective-permute-start.1 = (bf16[256,1024]{1,0:T(8,128)(2,1)S(1)}, bf16[256,1024]{1,0:T(8,128)(2,1)S(1)}, u32[]{:S(2)}, u32[]{:S(2)}) collective-permute-start(bf16[256,1024]{1,0:T(8,128)(2,1)S(1)} %get-tuple-element.7), channel_id=1, source_target_pairs={{0,1},{1,0},{2,3},{3,2},{4,5},{5,4},{6,7},{7,6}} | collective-permute-start | bytes 1572872 | tf_op jit(solution)/shard_map/ppermute | solution.py:334
  282.6 12.9 %collective-permute-start = (bf16[256,1024]{1,0:T(8,128)(2,1)S(1)}, bf16[256,1024]{1,0:T(8,128)(2,1)S(1)}, u32[]{:S(2)}, u32[]{:S(2)}) collective-permute-start(bf16[256,1024]{1,0:T(8,128)(2,1)S(1)} %get-tuple-element.7), channel_id=1, source_target_pairs={{0,4},{1,3},{2,6},{3,1},{4,0},{5,7},{6,2},{7,5}} | collective-permute-start | bytes 1572872 | tf_op jit(solution)/shard_map/ppermute | solution.py:334

commit v4 on v3

--- a/solution.py
+++ b/solution.py
@@ -10,7 +10,7 @@
 MESH = pl.DeviceIdType.MESH
 SLOTS = 4
 HELD = 8
-TAIL = 4
+TAIL = 5
 RAW = 4
 RS1, RS2, AG1, AG2, AG3 = 1, 2, 3, 5, 6
 
@@ -267,31 +267,35 @@
     return [pl.ds(pl.multiple_of(i, quarter), quarter) for i in starts]
 
 
-def spread(tail, held, o_ref, sem):
-    mats, d, ff = o_ref.shape
-    own = place(lax.axis_index("dp"), d)[0]
-    parts = [(n, pl.ds(i * (d // 4), d // 4), pl.ds(0, ff)) for n in range(mats - 1) for i in range(4)]
-    parts += [(mats - 1, pl.ds(i * (d // 4), d // 4), pl.ds(0, ff - tail)) for i in range(4)]
-    parts += [(mats - 1, own, pl.ds(ff - tail, tail))]
-    copies = [pltpu.make_async_copy(held.at[p], o_ref.at[p], sem.at[i]) for i, p in enumerate(parts)]
+def run(copies):
     for c in copies:
         c.start()
     for c in copies:
         c.wait()
 
 
+def spread(held, o_ref, sem):
+    mats, d, ff = o_ref.shape
+    parts = [(n, pl.ds(i * (d // 4), d // 4)) for n in range(mats - 1) for i in range(4)]
+    run([pltpu.make_async_copy(held.at[p], o_ref.at[p], sem.at[i]) for i, p in enumerate(parts)])
+
+
+def spread_last(tail, held, _, o_ref, sem):
+    mats, d, ff = o_ref.shape
+    own = place(lax.axis_index("dp"), d)[0]
+    parts = [(mats - 1, pl.ds(i * (d // 4), d // 4), pl.ds(0, ff - tail)) for i in range(4)]
+    parts += [(mats - 1, own, pl.ds(ff - tail, tail))]
+    run([pltpu.make_async_copy(held.at[p], o_ref.at[p], sem.at[i]) for i, p in enumerate(parts)])
+
+
 def finish(from_u, from_mate, from_far, _, o_ref, sem):
     mats, d, ff = o_ref.shape
     tail = from_u.shape[1]
     rows = place(lax.axis_index("dp"), d)[1:]
-    copies = [
+    run([
         pltpu.make_async_copy(piece, o_ref.at[mats - 1, r, pl.ds(ff - tail, tail)], sem.at[i])
         for i, (piece, r) in enumerate(zip((from_u, from_mate, from_far), rows))
-    ]
-    for c in copies:
-        c.start()
-    for c in copies:
-        c.wait()
+    ])
 
 
 def solution(mesh):
@@ -330,21 +334,32 @@
             ),
         )(a, g)
         devices = range(mesh.shape["dp"])
-        near = [flip(i, 2 if i % 2 else 4) for i in devices]
-        send = lambda to: lax.ppermute(quarters, "dp", [(i, to[i]) for i in devices])
-        from_u = send(near)
-        from_far = send([flip(i, 1) for i in near])
-        from_mate = send([flip(i, 1) for i in devices])
+        send = lambda x, to: lax.ppermute(x, "dp", [(i, to[i]) for i in devices])
+        mates = [flip(i, 1) for i in devices]
+        from_u = send(quarters, [flip(i, 2 if i % 2 else 4) for i in devices])
+        from_mate = send(quarters, mates)
+        from_far = send(from_u, mates)
         whole = jax.ShapeDtypeStruct((mats, d, ff), bf16)
+        cost = lambda n: pl.CostEstimate(flops=n * 10**10, bytes_accessed=2 * n * d * ff * 2, transcendentals=0)
         out = pl.pallas_call(
-            functools.partial(spread, tail),
+            spread,
             out_shape=whole,
             in_specs=[pl.BlockSpec(memory_space=pltpu.VMEM)],
             out_specs=pl.BlockSpec(memory_space=pl.ANY),
-            scratch_shapes=[dma((4 * mats + 1,))],
+            scratch_shapes=[dma((4 * mats,))],
             compiler_params=pltpu.CompilerParams(vmem_limit_bytes=2**20),
-            cost_estimate=pl.CostEstimate(flops=10**10, bytes_accessed=2 * mats * d * ff * 2, transcendentals=0),
+            cost_estimate=cost(mats - 1),
         )(held)
+        out = pl.pallas_call(
+            functools.partial(spread_last, tail),
+            out_shape=whole,
+            in_specs=[pl.BlockSpec(memory_space=pltpu.VMEM), pl.BlockSpec(memory_space=pl.ANY)],
+            out_specs=pl.BlockSpec(memory_space=pl.ANY),
+            scratch_shapes=[dma((5,))],
+            input_output_aliases={1: 0},
+            compiler_params=pltpu.CompilerParams(vmem_limit_bytes=2**20),
+            cost_estimate=cost(1),
+        )(held, out)
         return pl.pallas_call(
             finish,
             out_shape=whole,

time: 297 us -> 295 us (level)
    pallas_call x1 -> x2, Pallas kernels: 10.5 us -> 11.2 us  [the longest x1 8.51 us: step(): pl.pallas_call(spread, out_shape=whole, in_specs=[pl.BlockSpec(memory_spa...]
where the time goes in v4:
time: 295 us
  Pallas kernels  293 us (99%)
    pallas_call x1, Pallas kernels, step(): pl.pallas_call(functools.partial(kernel, (mats, tokens, d, ff, width, blo...  280 us
    pallas_call x1, Pallas kernels, step(): pl.pallas_call(spread, out_shape=whole, in_specs=[pl.BlockSpec(memory_spa...  8.51 us
  transfers between devices with their start and end apart: 3, of which 1 were waited for; matrix products, arithmetic and copies ran while one was open for 0% of the time, Pallas kernels for 4%

profile of v4, /device:TPU:0, one launch (start us, length us, event | category | flops | bytes accessed | tf_op | source)
XLA Modules:
  0.0 294.7 jit_solution(14652577595402169033)
XLA Ops:
  0.0 280.0 %shard_map.28 = (bf16[4,1024,4096]{2,1,0:T(8,128)(2,1)S(1)}, bf16[256,1280]{1,0:T(8,128)(2,1)S(1)}) custom-call(bf16[1,4,4096,1024]{3,2,1,0:T(8,128)(2,1)} %a_ref.1, bf16[1,4,4096,4096]{3,2,1,0:T(8,128)(2,1)} %g_ref.1), custom_call_target="tpu_custom_call" | custom-call | tf_op jit(solution)/shard_map/pallas_call | solution.py:311
  280.0 1.5 collective-permute-start
  281.6 0.0 collective-permute-start.1
  281.6 8.5 %shard_map.29._ = bf16[4,1024,4096]{2,1,0:T(8,128)(2,1)} custom-call(bf16[4,1024,4096]{2,1,0:T(8,128)(2,1)S(1)} %get-tuple-element.8.held), custom_call_target="tpu_custom_call" | custom-call | flops 30000001024 | bytes 50331648 | tf_op jit(solution)/shard_map/pallas_call | solution.py:344
  290.1 0.5 collective-permute-done.from_u
  290.7 0.0 collective-permute-start.2
  290.7 2.7 shard_map.30._
  293.4 0.0 collective-permute-done.1.from_mate
  293.4 0.0 collective-permute-done.2.from_far
  293.4 1.3 shard_map.31
Async XLA Ops:
  280.0 10.6 %collective-permute-start = (bf16[256,1280]{1,0:T(8,128)(2,1)S(1)}, bf16[256,1280]{1,0:T(8,128)(2,1)S(1)}, u32[]{:S(2)}, u32[]{:S(2)}) collective-permute-start(bf16[256,1280]{1,0:T(8,128)(2,1)S(1)} %get-tuple-element.7), channel_id=1, source_target_pairs={{0,4},{1,3},{2,6},{3,1},{4,0},{5,7},{6,2},{7,5}} | collective-permute-start | bytes 1966088 | tf_op jit(solution)/shard_map/ppermute | solution.py:337
  281.6 11.8 %collective-permute-start.1 = (bf16[256,1280]{1,0:T(8,128)(2,1)S(1)}, bf16[256,1280]{1,0:T(8,128)(2,1)S(1)}, u32[]{:S(2)}, u32[]{:S(2)}) collective-permute-start(bf16[256,1280]{1,0:T(8,128)(2,1)S(1)} %get-tuple-element.7), channel_id=1, source_target_pairs={{0,1},{1,0},{2,3},{3,2},{4,5},{5,4},{6,7},{7,6}} | collective-permute-start | bytes 1966088 | tf_op jit(solution)/shard_map/ppermute | solution.py:337
  290.7 2.8 collective-permute-start.2

commit v5 on v4

--- a/solution.py
+++ b/solution.py
@@ -7,6 +7,7 @@
 from jax.experimental.pallas import tpu as pltpu
 from jax.sharding import PartitionSpec as P
 
+EARLY = 5
 MESH = pl.DeviceIdType.MESH
 SLOTS = 4
 HELD = 8
@@ -134,9 +135,7 @@
             pl.when(jnp.logical_and(k >= 0, k < end))(lambda: f(k))
         return run
 
-    def events(s, p):
-        c = lanes(p)
-
+    def gathers(s, p):
         @at(s, AG3, steps - (TAIL + p) // 2)
         def _(k):
             ag3(k, p).wait()
@@ -156,6 +155,9 @@
             def _():
                 to = pl.ds(pl.multiple_of(tail * part_w, part_w), part_w)
                 tail_ref[:, to] = o_ref[mats - 1, rows_q, cols_of(k, p)]
+
+    def scatters(s, p):
+        c = lanes(p)
 
         @at(s, RS2)
         def _(k):
@@ -171,6 +173,10 @@
             rs2_out[i, :, c] = (keep1[i, e_send, c] + rs1_in[i, e_send, c].astype(f32)).astype(bf16)
             rs2(k, p).start()
             keep2[i, :, c] = keep1[i, e_keep, c] + rs1_in[i, e_keep, c].astype(f32)
+
+    def events(s, p):
+        gathers(s, p)
+        scatters(s, p)
 
     def send_on(s, product):
         d2d(s, 0).wait()
@@ -247,13 +253,16 @@
         d2d(s, 1).start()
         events(s, 0)
         send_on(s, lambda: product(send_mine))
+        pl.when(s <= EARLY)(lambda: events(s, 1))
         keep(s, lambda: product(keep_mine))
-        events(s, 1)
+        pl.when(s > EARLY)(lambda: events(s, 1))
 
     @pl.loop(steps, steps + AG3 + 1)
     def _(s):
-        events(s, 0)
-        events(s, 1)
+        scatters(s, 0)
+        scatters(s, 1)
+        gathers(s, 0)
+        gathers(s, 1)
 
 
 def place(me, d):

time: 295 us -> 294 us (level)
  no operation moved by 1% of the time
where the time goes in v5:
time: 294 us
  Pallas kernels  292 us (99%)
    pallas_call x1, Pallas kernels, step(): pl.pallas_call(functools.partial(kernel, (mats, tokens, d, ff, width, blo...  280 us
    pallas_call x1, Pallas kernels, step(): pl.pallas_call(spread, out_shape=whole, in_specs=[pl.BlockSpec(memory_spa...  8.51 us
  transfers between devices with their start and end apart: 3, of which 1 were waited for; matrix products, arithmetic and copies ran while one was open for 0% of the time, Pallas kernels for 4%

profile of v5, /device:TPU:0, one launch (start us, length us, event | category | flops | bytes accessed | tf_op | source)
XLA Modules:
  0.0 294.3 jit_solution(9869384627364722165)
XLA Ops:
  0.0 279.6 %shard_map.28 = (bf16[4,1024,4096]{2,1,0:T(8,128)(2,1)S(1)}, bf16[256,1280]{1,0:T(8,128)(2,1)S(1)}) custom-call(bf16[1,4,4096,1024]{3,2,1,0:T(8,128)(2,1)} %a_ref.1, bf16[1,4,4096,4096]{3,2,1,0:T(8,128)(2,1)} %g_ref.1), custom_call_target="tpu_custom_call" | custom-call | tf_op jit(solution)/shard_map/pallas_call | solution.py:320
  279.6 1.5 collective-permute-start
  281.1 0.0 collective-permute-start.1
  281.1 8.5 %shard_map.29._ = bf16[4,1024,4096]{2,1,0:T(8,128)(2,1)} custom-call(bf16[4,1024,4096]{2,1,0:T(8,128)(2,1)S(1)} %get-tuple-element.8.held), custom_call_target="tpu_custom_call" | custom-call | flops 30000001024 | bytes 50331648 | tf_op jit(solution)/shard_map/pallas_call | solution.py:353
  289.6 0.6 collective-permute-done.from_u
  290.2 0.0 collective-permute-start.2
  290.2 2.7 shard_map.30._
  293.0 0.0 collective-permute-done.1.from_mate
  293.0 0.0 collective-permute-done.2.from_far
  293.0 1.3 shard_map.31
Async XLA Ops:
  279.6 10.6 %collective-permute-start = (bf16[256,1280]{1,0:T(8,128)(2,1)S(1)}, bf16[256,1280]{1,0:T(8,128)(2,1)S(1)}, u32[]{:S(2)}, u32[]{:S(2)}) collective-permute-start(bf16[256,1280]{1,0:T(8,128)(2,1)S(1)} %get-tuple-element.7), channel_id=1, source_target_pairs={{0,4},{1,3},{2,6},{3,1},{4,0},{5,7},{6,2},{7,5}} | collective-permute-start | bytes 1966088 | tf_op jit(solution)/shard_map/ppermute | solution.py:346
  281.1 11.9 %collective-permute-start.1 = (bf16[256,1280]{1,0:T(8,128)(2,1)S(1)}, bf16[256,1280]{1,0:T(8,128)(2,1)S(1)}, u32[]{:S(2)}, u32[]{:S(2)}) collective-permute-start(bf16[256,1280]{1,0:T(8,128)(2,1)S(1)} %get-tuple-element.7), channel_id=1, source_target_pairs={{0,1},{1,0},{2,3},{3,2},{4,5},{5,4},{6,7},{7,6}} | collective-permute-start | bytes 1966088 | tf_op jit(solution)/shard_map/ppermute | solution.py:346
  290.2 2.8 collective-permute-start.2
